TPU v7x, 32 devices: a whole 2x2x4 slice. The times are simulated.
32 devices in a mesh: rep: 16 (over z, y, core), grp: 2 (over x).
Axes of the slice: x: 2, y: 2, z: 4, core: 2. Of those that a mesh axis runs over, the one named last changes fastest.
Arguments:
- local_params: bfloat16 [16, 2, 32, 8192], P('rep', 'grp'), may hold values from -130 to 130
- snapshot: bfloat16 [2, 32, 8192], P('grp'), may hold values from -4 to 4
- master: float32 [2, 32, 8192], P('grp', 'rep'), may hold values from -6 to 6
- momentum: float32 [2, 32, 8192], P('grp', 'rep'), may hold values from -4 to 4
Outputs:
- new_master: float32 [2, 32, 8192], P('grp', 'rep')
- new_momentum: float32 [2, 32, 8192], P('grp', 'rep')
- new_params: bfloat16 [2, 32, 8192], P('grp')
All inputs are finite; a program needn't handle non-finite values.
Results may differ from a plain program's by a relative error of at most 0.001.
Values may be sent and summed in bfloat16 or wider, within the bound.
A program may use at most 128 MiB of HBM per device.

v0:
```python
import jax
import jax.numpy as jnp
from jax import lax
from jax.sharding import PartitionSpec as P

nesterov_mu = 0.9
outer_rate = 0.7
clip_limit = 0.15
epsilon = 1e-06


def body(local_params, snapshot, master, momentum):
    replicas = lax.axis_size("rep")
    own_rows = master.shape[1]
    replica_sum = jnp.sum(
        lax.all_to_all(local_params[0], "rep", split_axis=1, concat_axis=0, tiled=True).astype(
            jnp.float32
        ),
        axis=0,
        keepdims=True,
    )
    owned_snap = lax.dynamic_slice_in_dim(
        snapshot, lax.axis_index("rep") * own_rows, own_rows, 1
    ).astype(jnp.float32)
    outer_grad = owned_snap - replica_sum / replicas
    elements = snapshot.shape[1] * snapshot.shape[2] * lax.axis_size("grp")
    squares = lax.psum(jnp.sum(outer_grad * outer_grad), ("rep", "grp"))
    grad_rms = jnp.sqrt(squares / elements + epsilon)
    clipped = jnp.minimum(1.0, clip_limit / grad_rms) * outer_grad
    new_momentum = nesterov_mu * momentum + clipped
    new_master = master - outer_rate * (clipped + nesterov_mu * new_momentum)
    new_params = lax.all_gather(new_master.astype(jnp.bfloat16), "rep", axis=1, tiled=True)
    return (new_master, new_momentum, new_params)


def solution(mesh):
    return jax.shard_map(
        body,
        mesh=mesh,
        in_specs=(
            P("rep", "grp", None, None),
            P("grp", None, None),
            P("grp", "rep", None),
            P("grp", "rep", None),
        ),
        out_specs=(P("grp", "rep", None), P("grp", "rep", None), P("grp", None, None)),
        check_vma=False,
    )
```

profile of v0, /device:TPU:0, one launch (start us, length us, event | category | flops | bytes accessed | tf_op | source)
XLA Modules:
  0.0 102.9 jit_solution(10499969501519827075)
XLA Ops:
  0.6 0.0 copy-start
  0.6 2.2 %copy.40 = bf16[1,32,8192]{2,0,1:T(2,128)(2,1)S(1)} copy(bf16[1,32,8192]{2,1,0:T(8,128)(2,1)} %bitcast.7) | data formatting | bytes 1048576 | tf_op jit(solution)/shard_map/squeeze | solution.py:16
  2.9 0.5 broadcast.18
  3.4 3.8 %reduce.2 = bf16[32,8192]{1,0:T(8,128)(2,1)S(1)} reduce(bf16[32,1,8192]{2,1,0:T(2,128)(2,1)S(1)} %bitcast.6, bf16[]{:T(256)} %broadcast.18), dimensions={1}, to_apply=%bitcast.5.reduce_sub_computation | reduce | bytes 1048578
  7.2 1.1 %reshape.23 = bf16[16,2,8192]{2,1,0:T(2,128)(2,1)} reshape(bf16[32,8192]{1,0:T(8,128)(2,1)S(1)} %reduce.2) | data formatting | bytes 1048576
  8.3 7.4 %all-to-all-start = ((bf16[16,2,8192]{2,1,0:T(2,128)(2,1)}), bf16[16,2,8192]{2,1,0:T(2,128)(2,1)S(1)}, u32[]{:S(2)}, u32[]{:S(2)}) async-start(bf16[16,2,8192]{2,1,0:T(2,128)(2,1)} %reshape.23), calls=%async_computation | async-start | bytes 1048576 | tf_op jit(solution)/shard_map/all_to_all | solution.py:16
  15.7 0.0 copy-done
  15.8 14.2 %all-to-all-done = bf16[16,2,8192]{2,1,0:T(2,128)(2,1)S(1)} async-done(((bf16[16,2,8192]{2,1,0:T(2,128)(2,1)}), bf16[16,2,8192]{2,1,0:T(2,128)(2,1)S(1)}, u32[]{:S(2)}, u32[]{:S(2)}) %all-to-all-start) | async-done | bytes 524320 | tf_op jit(solution)/shard_map/all_to_all | solution.py:16
  30.0 0.5 reshape.24
  30.5 3.0 %convert_reduce_fusion = f32[32,8192]{1,0:T(8,128)S(1)} fusion(bf16[32,1,8192]{2,1,0:T(2,128)(2,1)S(1)} %reshape.24), kind=kLoop, calls=%fused_computation | loop fusion | flops 262144 | bytes 1572864 | tf_op jit(solution)/shard_map/convert_element_type | solution.py:16
  33.6 0.6 reshape.21
  34.2 0.4 reduce_sum.18
  34.6 0.0 copy-start.1
  34.6 0.7 multiply_reduce_fusion
  35.4 0.1 copy-done.1
  35.5 0.0 copy-start.2
  35.5 39.8 %psum.7 = f32[]{:T(128)} all-reduce(f32[]{:T(128)} %multiply_reduce_fusion), channel_id=1, replica_groups=mesh['rep'=16,'grp'=2] {'rep','grp'}, use_global_device_ids=true, to_apply=%region_2.0 | all-reduce | flops 1 | bytes 8 | tf_op jit(solution)/shard_map/psum | solution.py:27
  76.0 0.0 copy-done.2
  76.0 0.2 fusion.1
  76.3 0.7 copy.19
  76.9 0.7 copy.20
  77.6 23.9 %all_gather.3 = bf16[1,32,8192]{2,0,1:T(2,128)(2,1)S(1)} all-gather(bf16[1,2,8192]{2,0,1:T(2,128)(2,1)S(1)} %get-tuple-element.9), channel_id=1, replica_groups=mesh['rep'=16,'grp'=2] {'rep'}, dimensions={1}, use_global_device_ids=true | all-gather | bytes 557056 | tf_op jit(solution)/shard_map/all_gather | solution.py:32
  101.5 1.4 %copy.21 = bf16[1,32,8192]{2,1,0:T(8,128)(2,1)} copy(bf16[1,32,8192]{2,0,1:T(2,128)(2,1)S(1)} %all_gather.3) | data formatting | bytes 1048576
  (3 shorter events, 0.1 us)
Async XLA Ops:
  0.6 15.1 %copy-start = (bf16[1,32,8192]{2,1,0:T(8,128)(2,1)S(1)}, bf16[1,32,8192]{2,1,0:T(8,128)(2,1)}, u32[]{:S(2)}) copy-start(bf16[1,32,8192]{2,1,0:T(8,128)(2,1)} %param.5) | copy-start | bytes 1572868
  8.3 21.7 %all-to-all-start = ((bf16[16,2,8192]{2,1,0:T(2,128)(2,1)}), bf16[16,2,8192]{2,1,0:T(2,128)(2,1)S(1)}, u32[]{:S(2)}, u32[]{:S(2)}) async-start(bf16[16,2,8192]{2,1,0:T(2,128)(2,1)} %reshape.23), calls=%async_computation | async-start | bytes 1048576 | tf_op jit(solution)/shard_map/all_to_all | solution.py:16
  34.6 0.8 copy-start.1
  35.5 40.5 %copy-start.2 = (f32[1,2,8192]{2,1,0:T(2,128)S(1)}, f32[1,2,8192]{2,1,0:T(2,128)}, u32[]{:S(2)}) copy-start(f32[1,2,8192]{2,1,0:T(2,128)} %param.6) | copy-start | bytes 196612
where the time goes:
time: 103 us
  blocking collectives  63.7 us (62%)
  waiting for transfers between devices  14.2 us (14%)
  other arithmetic  8.25 us (8%)
  local copies, waits for them, and re-layouts  7.88 us (8%)
  starting transfers between devices  7.41 us (7%)
  between operations  1.45 us (1%)
    psum x1, blocking collectives, body(): squares = lax.psum(jnp.sum(outer_grad * outer_grad), ('rep', 'grp'))  39.8 us
    all_gather x1, blocking collectives, body(): lax.all_gather(new_master.astype(jnp.bfloat16), 'rep', axis=1, tiled=True)  23.9 us
    all_to_all x1, waiting for transfers between devices, body(): lax.all_to_all(local_params[0], 'rep', split_axis=1, concat_axis=0, tiled...  14.2 us
    all_to_all x1, starting transfers between devices, body(): lax.all_to_all(local_params[0], 'rep', split_axis=1, concat_axis=0, tiled...  7.41 us
    unnamed x12, local copies, waits for them, and re-layouts  5.01 us
    unnamed x1, other arithmetic  3.81 us
    convert_element_type x1, other arithmetic, body(): lax.all_to_all(local_params[0], 'rep', split_axis=1, concat_axis=0, tiled...  3.02 us
    squeeze x1, local copies, waits for them, and re-layouts, body(): local_params[0]  2.2 us
  transfers between devices with their start and end apart: 1, of which 1 were waited for; matrix products, arithmetic and copies ran while one was open for 0% of the time, Pallas kernels for 0%

commit v1 on v0

--- a/solution.py
+++ b/solution.py
@@ -13,9 +13,15 @@
     replicas = lax.axis_size("rep")
     own_rows = master.shape[1]
     replica_sum = jnp.sum(
-        lax.all_to_all(local_params[0], "rep", split_axis=1, concat_axis=0, tiled=True).astype(
-            jnp.float32
-        ),
+        jnp.concatenate(
+            lax.all_to_all(
+                jnp.stack(jnp.split(local_params[0], lax.axis_size("rep"), axis=1), axis=0),
+                axis_name="rep",
+                split_axis=0,
+                concat_axis=0,
+            ),
+            axis=0,
+        ).astype(jnp.float32),
         axis=0,
         keepdims=True,
     )

time: 103 us -> 109 us (1.058)
  local copies, waits for them, and re-layouts: 7.88 us -> 20.5 us
  other arithmetic: 8.25 us -> 1.47 us
    unnamed x12 -> x26, local copies, waits for them, and re-layouts: 5.01 us -> 19.9 us
    unnamed x1 -> x0, other arithmetic: 3.81 us -> none
    convert_element_type x1 -> x0, other arithmetic: 3.02 us -> none  [body(): lax.all_to_all(local_params[0], 'rep', split_axis=1, concat_axis=0, tiled...]
    squeeze x1 -> x0, local copies, waits for them, and re-layouts: 2.2 us -> none  [body(): local_params[0]]
where the time goes in v1:
time: 109 us
  blocking collectives  63.7 us (58%)
  local copies, waits for them, and re-layouts  20.5 us (19%)
  waiting for transfers between devices  14.2 us (13%)
  starting transfers between devices  7.41 us (7%)
  other arithmetic  1.47 us (1%)
  between operations  1.42 us (1%)
    psum x1, blocking collectives, body(): squares = lax.psum(jnp.sum(outer_grad * outer_grad), ('rep', 'grp'))  39.8 us
    all_gather x1, blocking collectives, body(): lax.all_gather(new_master.astype(jnp.bfloat16), 'rep', axis=1, tiled=True)  23.9 us
    unnamed x26, local copies, waits for them, and re-layouts  19.9 us
    all_to_all x1, waiting for transfers between devices, body(): lax.all_to_all(jnp.stack(jnp.split(local_params[0], lax.axis_size('rep'),...  14.2 us
    all_to_all x1, starting transfers between devices, body(): lax.all_to_all(jnp.stack(jnp.split(local_params[0], lax.axis_size('rep'),...  7.41 us
  transfers between devices with their start and end apart: 1, of which 1 were waited for; matrix products, arithmetic and copies ran while one was open for 0% of the time, Pallas kernels for 0%

profile of v1, /device:TPU:0, one launch (start us, length us, event | category | flops | bytes accessed | tf_op | source)
XLA Modules:
  0.0 108.8 jit_solution(14995001041123533205)
XLA Ops:
  0.6 0.0 copy-start
  0.6 0.0 copy-start.1
  0.7 1.6 %constant_dynamic-update-slice_fusion.15 = bf16[16,1,2,8192]{3,2,1,0:T(2,128)(2,1)} fusion(bf16[1,32,8192]{2,1,0:T(8,128)(2,1)} %bitcast.65), kind=kLoop, calls=%fused_computation.21 | loop fusion | bytes 65536
  2.3 1.6 %constant_dynamic-update-slice_fusion.14 = bf16[16,1,2,8192]{3,2,1,0:T(2,128)(2,1)} fusion(bf16[16,1,2,8192]{3,2,1,0:T(2,128)(2,1)} %constant_dynamic-update-slice_fusion.15, bf16[1,32,8192]{2,1,0:T(8,128)(2,1)} %bitcast.66), kind=kLoop, calls=%fused_computation.20 | loop fusion | bytes 65536
  3.8 1.6 %constant_dynamic-update-slice_fusion.13 = bf16[16,1,2,8192]{3,2,1,0:T(2,128)(2,1)} fusion(bf16[16,1,2,8192]{3,2,1,0:T(2,128)(2,1)} %constant_dynamic-update-slice_fusion.14, bf16[1,32,8192]{2,1,0:T(8,128)(2,1)} %bitcast.67), kind=kLoop, calls=%fused_computation.19 | loop fusion | bytes 65536
  5.4 1.6 %constant_dynamic-update-slice_fusion.12 = bf16[16,1,2,8192]{3,2,1,0:T(2,128)(2,1)} fusion(bf16[16,1,2,8192]{3,2,1,0:T(2,128)(2,1)} %constant_dynamic-update-slice_fusion.13, bf16[1,32,8192]{2,1,0:T(8,128)(2,1)} %bitcast.68), kind=kLoop, calls=%fused_computation.18 | loop fusion | bytes 65536
  6.9 1.5 %constant_dynamic-update-slice_fusion.11 = bf16[16,1,2,8192]{3,2,1,0:T(2,128)(2,1)} fusion(bf16[16,1,2,8192]{3,2,1,0:T(2,128)(2,1)} %constant_dynamic-update-slice_fusion.12, bf16[1,32,8192]{2,1,0:T(8,128)(2,1)} %bitcast.69), kind=kLoop, calls=%fused_computation.17 | loop fusion | bytes 65536
  8.5 1.6 %constant_dynamic-update-slice_fusion.10 = bf16[16,1,2,8192]{3,2,1,0:T(2,128)(2,1)} fusion(bf16[16,1,2,8192]{3,2,1,0:T(2,128)(2,1)} %constant_dynamic-update-slice_fusion.11, bf16[1,32,8192]{2,1,0:T(8,128)(2,1)} %bitcast.70), kind=kLoop, calls=%fused_computation.16 | loop fusion | bytes 65536
  10.0 1.6 %constant_dynamic-update-slice_fusion.9 = bf16[16,1,2,8192]{3,2,1,0:T(2,128)(2,1)} fusion(bf16[16,1,2,8192]{3,2,1,0:T(2,128)(2,1)} %constant_dynamic-update-slice_fusion.10, bf16[1,32,8192]{2,1,0:T(8,128)(2,1)} %bitcast.71), kind=kLoop, calls=%fused_computation.15 | loop fusion | bytes 65536
  11.6 1.6 %constant_dynamic-update-slice_fusion.8 = bf16[16,1,2,8192]{3,2,1,0:T(2,128)(2,1)} fusion(bf16[16,1,2,8192]{3,2,1,0:T(2,128)(2,1)} %constant_dynamic-update-slice_fusion.9, bf16[1,32,8192]{2,1,0:T(8,128)(2,1)} %bitcast.72), kind=kLoop, calls=%fused_computation.14 | loop fusion | bytes 65536
  13.1 0.0 copy-done.1
  13.1 0.6 constant_dynamic-update-slice_fusion.7
  13.8 0.7 constant_dynamic-update-slice_fusion.6
  14.4 0.7 constant_dynamic-update-slice_fusion.5
  15.1 0.7 constant_dynamic-update-slice_fusion.4
  15.7 0.6 constant_dynamic-update-slice_fusion.3
  16.4 0.7 constant_dynamic-update-slice_fusion.2
  17.0 0.7 constant_dynamic-update-slice_fusion.1
  17.7 0.7 constant_dynamic-update-slice_fusion
  18.3 7.4 %all-to-all-start = ((bf16[16,1,2,8192]{3,2,1,0:T(2,128)(2,1)}), bf16[16,1,2,8192]{3,2,1,0:T(2,128)(2,1)S(1)}, u32[]{:S(2)}, u32[]{:S(2)}) async-start(bf16[16,1,2,8192]{3,2,1,0:T(2,128)(2,1)} %constant_dynamic-update-slice_fusion), calls=%async_computation | async-start | bytes 1048576 | tf_op jit(solution)/shard_map/all_to_all | solution.py:17
  25.7 0.0 copy-done
  25.8 14.2 %all-to-all-done = bf16[16,1,2,8192]{3,2,1,0:T(2,128)(2,1)S(1)} async-done(((bf16[16,1,2,8192]{3,2,1,0:T(2,128)(2,1)}), bf16[16,1,2,8192]{3,2,1,0:T(2,128)(2,1)S(1)}, u32[]{:S(2)}, u32[]{:S(2)}) %all-to-all-start) | async-done | bytes 524320 | tf_op jit(solution)/shard_map/all_to_all | solution.py:17
  40.0 0.4 convert_reduce_fusion
  40.5 0.0 copy-start.2
  40.5 0.7 multiply_reduce_fusion
  41.2 0.1 copy-done.2
  41.4 39.8 %psum.7 = f32[]{:T(128)} all-reduce(f32[]{:T(128)} %multiply_reduce_fusion), channel_id=1, replica_groups=mesh['rep'=16,'grp'=2] {'rep','grp'}, use_global_device_ids=true, to_apply=%region_2.0 | all-reduce | flops 1 | bytes 8 | tf_op jit(solution)/shard_map/psum | solution.py:33
  81.9 0.2 fusion.1
  82.1 0.7 copy.11
  82.8 0.7 copy.12
  83.5 23.9 %all_gather.3 = bf16[1,32,8192]{2,0,1:T(2,128)(2,1)S(1)} all-gather(bf16[1,2,8192]{2,0,1:T(2,128)(2,1)S(1)} %get-tuple-element.6), channel_id=1, replica_groups=mesh['rep'=16,'grp'=2] {'rep'}, dimensions={1}, use_global_device_ids=true | all-gather | bytes 557056 | tf_op jit(solution)/shard_map/all_gather | solution.py:38
  107.4 1.4 %copy.13 = bf16[1,32,8192]{2,1,0:T(8,128)(2,1)} copy(bf16[1,32,8192]{2,0,1:T(2,128)(2,1)S(1)} %all_gather.3) | data formatting | bytes 1048576
  (5 shorter events, 0.1 us)
Async XLA Ops:
  0.6 25.1 %copy-start = (bf16[1,32,8192]{2,1,0:T(8,128)(2,1)S(1)}, bf16[1,32,8192]{2,1,0:T(8,128)(2,1)}, u32[]{:S(2)}) copy-start(bf16[1,32,8192]{2,1,0:T(8,128)(2,1)} %param.5) | copy-start | bytes 1572868
  0.6 12.5 %copy-start.1 = (bf16[1,1,32,8192]{3,2,1,0:T(8,128)(2,1)S(1)}, bf16[1,1,32,8192]{3,2,1,0:T(8,128)(2,1)}, u32[]{:S(2)}) copy-start(bf16[1,1,32,8192]{3,2,1,0:T(8,128)(2,1)} %param.4) | copy-start | bytes 1572868
  18.3 21.7 %all-to-all-start = ((bf16[16,1,2,8192]{3,2,1,0:T(2,128)(2,1)}), bf16[16,1,2,8192]{3,2,1,0:T(2,128)(2,1)S(1)}, u32[]{:S(2)}, u32[]{:S(2)}) async-start(bf16[16,1,2,8192]{3,2,1,0:T(2,128)(2,1)} %constant_dynamic-update-slice_fusion), calls=%async_computation | async-start | bytes 1048576 | tf_op jit(solution)/shard_map/all_to_all | solution.py:17
  40.5 0.8 copy-start.2
  41.3 40.5 %copy-start.3 = (f32[1,2,8192]{2,1,0:T(2,128)S(1)}, f32[1,2,8192]{2,1,0:T(2,128)}, u32[]{:S(2)}) copy-start(f32[1,2,8192]{2,1,0:T(2,128)} %param.6) | copy-start | bytes 196612
